TPU v7x, 32 devices: a whole 2x2x4 slice. The times are simulated.
32 devices in a mesh: row: 4 (over x, core), col: 4 (over z), pt: 2 (over y).
Axes of the slice: x: 2, y: 2, z: 4, core: 2. Of those that a mesh axis runs over, the one named last changes fastest.
Arguments:
- first_factors: int32 [32, 1024, 1024], P('pt', 'row', 'col'), may hold values from 0 to 12288
- second_factors: int32 [32, 1024, 1024], P('pt', 'row', 'col'), may hold values from 0 to 12288
Outputs:
- scaled_product: float32 [45, 1024, 1024], P(None, ('row', 'pt'), 'col')
All inputs are finite; a program needn't handle non-finite values.
Results may differ from a plain program's by a relative error of at most 0.0003.
Values may be sent and summed in bfloat16 or wider, within the bound.
A program may use at most 128 MiB of HBM per device.

v0:
```python
import jax
import jax.numpy as jnp
import numpy as np
from jax import lax
from jax.sharding import PartitionSpec as P

DEG = 16


modulus = 12289
digit_base = 128


def primitive_root():
    for candidate in range(2, modulus):
        if pow(candidate, 6144, modulus) != 1 and pow(candidate, 4096, modulus) != 1:
            return candidate
    return 0


def make_table(order_size, row_count, column_count, inverse):
    generator = primitive_root()
    root_value = pow(generator, (modulus - 1) // order_size, modulus)
    scaling = 1
    if inverse:
        root_value = pow(root_value, modulus - 2, modulus)
        scaling = pow(order_size, modulus - 2, modulus)
    entries = [
        [
            pow(root_value, row_index * column_index % order_size, modulus) * scaling % modulus
            for column_index in range(column_count)
        ]
        for row_index in range(row_count)
    ]
    return np.array(entries, dtype=np.int64)


def value_digits(values):
    high_digit = values // digit_base
    return (
        high_digit.astype(jnp.bfloat16),
        (values - digit_base * high_digit).astype(jnp.bfloat16),
    )


def combine(high_high, high_low, low_high, low_low):
    top_part = high_high.astype(jnp.int32) % modulus
    middle_part = (high_low.astype(jnp.int32) + low_high.astype(jnp.int32)) % modulus
    return (
        top_part * (digit_base * digit_base) % modulus
        + middle_part * digit_base
        + low_low.astype(jnp.int32)
    ) % modulus


def transform(matrix_table, coefs):
    slot_count = coefs.shape[0]
    flat_coefs = coefs.reshape(slot_count, -1)
    table_high = jnp.asarray(matrix_table // digit_base, dtype=jnp.bfloat16)
    table_low = jnp.asarray(matrix_table % digit_base, dtype=jnp.bfloat16)
    data_high, data_low = value_digits(flat_coefs)

    def product_of(left_part, right_part):
        return jnp.dot(left_part, right_part, preferred_element_type=jnp.float32)

    mixed_values = combine(
        product_of(table_high, data_high),
        product_of(table_high, data_low),
        product_of(table_low, data_high),
        product_of(table_low, data_low),
    )
    return mixed_values.reshape(matrix_table.shape[0], coefs.shape[1], coefs.shape[2])


def batched_product(left_part, right_part):
    return jnp.einsum("bik,bkj->bij", left_part, right_part, preferred_element_type=jnp.float32)


def digit_sum(totals, left_digits, right_digits):
    return (
        totals[0] + batched_product(left_digits[0], right_digits[0]),
        totals[1] + batched_product(left_digits[0], right_digits[1]),
        totals[2] + batched_product(left_digits[1], right_digits[0]),
        totals[3] + batched_product(left_digits[1], right_digits[1]),
    )


def pointwise(left_values, right_values):
    left_points, right_points = (
        lax.all_to_all(
            lax.all_to_all(
                left_values.astype(jnp.float32), "col", split_axis=0, concat_axis=2, tiled=True
            ),
            "pt",
            split_axis=0,
            concat_axis=1,
            tiled=True,
        ),
        lax.all_to_all(
            lax.all_to_all(
                right_values.astype(jnp.float32), "col", split_axis=0, concat_axis=2, tiled=True
            ),
            "pt",
            split_axis=0,
            concat_axis=1,
            tiled=True,
        ),
    )
    left_digits = value_digits(left_points.astype(jnp.int32))
    right_digits = value_digits(right_points.astype(jnp.int32))
    zeros_init = jnp.zeros(left_points.shape, jnp.float32)
    column_parts = tuple((digit_part for digit_part in left_digits))
    totals = digit_sum(
        (zeros_init, zeros_init, zeros_init, zeros_init),
        column_parts,
        (
            lax.all_gather(right_digits[0], "row", axis=1, tiled=True),
            lax.all_gather(right_digits[1], "row", axis=1, tiled=True),
        ),
    )
    product_values = combine(totals[0], totals[1], totals[2], totals[3]).astype(jnp.float32)
    arrived = lax.all_to_all(
        lax.all_to_all(product_values, "col", split_axis=2, concat_axis=0, tiled=True),
        "pt",
        split_axis=1,
        concat_axis=0,
        tiled=True,
    )
    col_count = lax.axis_size("col")
    pt_count = lax.axis_size("pt")
    local_count = arrived.shape[0] // (col_count * pt_count)
    returned = arrived.reshape(pt_count, col_count, local_count, arrived.shape[1], arrived.shape[2])
    returned = returned.transpose(1, 0, 2, 3, 4).reshape(arrived.shape)
    return returned.astype(jnp.int32)


def local(first_factors, second_factors):
    forward_one = make_table(2 * DEG, 2 * DEG, DEG, False)
    inverse_one = make_table(2 * DEG, 2 * DEG, 2 * DEG, True)
    forward_two = make_table(4 * DEG, 4 * DEG, 2 * DEG, False)
    inverse_two = make_table(4 * DEG, 3 * DEG - 3, 4 * DEG, True)
    first_entries, second_entries = (
        lax.all_to_all(
            first_factors.astype(jnp.float32), "pt", split_axis=1, concat_axis=0, tiled=True
        ),
        lax.all_to_all(
            second_factors.astype(jnp.float32), "pt", split_axis=1, concat_axis=0, tiled=True
        ),
    )
    first_entries = first_entries.astype(jnp.int32)
    second_entries = second_entries.astype(jnp.int32)
    left_values = jnp.concatenate(
        [transform(forward_one, first_entries[:DEG]), transform(forward_one, first_entries[DEG:])],
        0,
    )
    right_values = jnp.concatenate(
        [
            transform(forward_one, second_entries[:DEG]),
            transform(forward_one, second_entries[DEG:]),
        ],
        0,
    )
    products = pointwise(left_values, right_values)
    first_product = transform(inverse_one, products[: 2 * DEG])
    second_product = transform(inverse_one, products[2 * DEG :])
    upper_values = transform(forward_two, first_product)
    lower_values = transform(forward_two[:, :DEG], second_product[DEG:])
    result_coefficients = transform(inverse_two, pointwise(upper_values, lower_values))
    return result_coefficients.astype(jnp.float32) / 12289.0


def reduce_centred(values):
    return values - 12289.0 * jnp.round(values * (1.0 / 12289.0))


def centred_digits(values):
    high_digit = jnp.round(values * (1.0 / 128.0))
    return high_digit.astype(jnp.bfloat16), (values - 128.0 * high_digit).astype(jnp.bfloat16)


def combine_centred(high_high, middle, low_low):
    upper_part = reduce_centred(reduce_centred(high_high) * 128.0 + middle)
    return reduce_centred(upper_part * 128.0 + low_low)


def table_digits(matrix_table):
    centred = np.where(matrix_table > modulus // 2, matrix_table - modulus, matrix_table)
    high_digit = np.round(centred / 128.0)
    return high_digit, centred - 128.0 * high_digit


def centred_transform(table_high, table_low, coefs):
    data_high, data_low = centred_digits(coefs.astype(jnp.float32))
    table_high = jnp.asarray(table_high, dtype=jnp.bfloat16)
    table_low = jnp.asarray(table_low, dtype=jnp.bfloat16)

    def product_of(left_part, right_part):
        return jnp.einsum("ts,sab->tab", left_part, right_part, preferred_element_type=jnp.float32)

    middle = product_of(
        jnp.concatenate([table_high, table_low], 1), jnp.concatenate([data_low, data_high], 0)
    )
    return combine_centred(
        product_of(table_high, data_high), middle, product_of(table_low, data_low)
    )


def column_pointwise(left_values, right_values):
    right_points = lax.all_to_all(
        right_values.astype(jnp.int16), "col", split_axis=0, concat_axis=2, tiled=True
    )
    right_points = lax.all_gather(right_points, "row", axis=1, tiled=True)
    left_points = lax.all_to_all(
        left_values.astype(jnp.int16), "col", split_axis=0, concat_axis=2, tiled=True
    )
    left_high, left_low = centred_digits(left_points.astype(jnp.float32))
    right_high, right_low = centred_digits(right_points.astype(jnp.float32))
    middle = batched_product(left_high, right_low) + batched_product(left_low, right_high)
    product_values = combine_centred(
        batched_product(left_high, right_high), middle, batched_product(left_low, right_low)
    )
    return lax.all_to_all(
        product_values.astype(jnp.int16), "col", split_axis=2, concat_axis=0, tiled=True
    )


def pair_local(first_factors, second_factors):
    forward_one = table_digits(make_table(2 * DEG, 2 * DEG, DEG, False))
    inverse_one = table_digits(make_table(2 * DEG, 2 * DEG, 2 * DEG, True))
    forward_two = table_digits(make_table(4 * DEG, 4 * DEG, 2 * DEG, False))
    inverse_two = table_digits(make_table(4 * DEG, 3 * DEG - 3, 4 * DEG, True))
    half_points = 2 * DEG
    place = lax.axis_index("pt")
    products = column_pointwise(
        centred_transform(*forward_one, centre(first_factors)),
        centred_transform(*forward_one, centre(second_factors)),
    )
    own_product = centred_transform(*inverse_one, products).astype(jnp.int16)
    both_products = lax.all_gather(own_product, "pt", axis=0, tiled=True)
    first_product = both_products[: 2 * DEG]
    shifted = both_products[3 * DEG :]
    own_tables = [
        lax.dynamic_slice_in_dim(
            jnp.asarray(digit, dtype=jnp.bfloat16), place * half_points, half_points, 0
        )
        for digit in forward_two
    ]
    upper_values = centred_transform(*own_tables, first_product)
    lower_values = centred_transform(*[digit[:, :DEG] for digit in own_tables], shifted)
    products_two = column_pointwise(upper_values, lower_values)
    all_points = lax.all_to_all(products_two, "pt", split_axis=1, concat_axis=0, tiled=True)
    result = centred_transform(*inverse_two, all_points)
    return jnp.where(result < 0.0, result + 12289.0, result) / 12289.0


def centre(values):
    return jnp.where(values > modulus // 2, values - modulus, values)


def solution(mesh):
    in_specs = (P("pt", "row", "col"), P("pt", "row", "col"))
    out_specs = P(None, ("row", "pt"), "col")
    body = pair_local if mesh.shape["pt"] == 2 else local
    return jax.shard_map(body, mesh=mesh, in_specs=in_specs, out_specs=out_specs, check_vma=False)
```

profile of v0, /device:TPU:4, one launch (start us, length us, event | category | flops | bytes accessed | tf_op | source)
XLA Modules:
  0.0 1256.2 jit_solution(4259190581243966023)
XLA Ops:
  44.4 73.9 %all-to-all-done = s16[32,256,256]{2,1,0:T(8,128)(2,1)} async-done(((s16[32,256,256]{2,1,0:T(8,128)(2,1)}), s16[32,256,256]{2,1,0:T(8,128)(2,1)}, u32[]{:S(2)}, u32[]{:S(2)}) %all-to-all-start) | async-done | bytes 4194336 | tf_op jit(solution)/shard_map/all_to_all | solution.py:213
  130.4 12.0 copy.111
  142.4 10.8 reshape.16
  153.2 63.1 %all-to-all-done.1 = s16[32,256,256]{2,1,0:T(8,128)(2,1)} async-done(((s16[32,256,256]{2,1,0:T(8,128)(2,1)}), s16[32,256,256]{2,1,0:T(8,128)(2,1)}, u32[]{:S(2)}, u32[]{:S(2)}) %all-to-all-start.1) | async-done | bytes 4194336 | tf_op jit(solution)/shard_map/all_to_all | solution.py:209
  216.3 7.4 copy.113
  223.7 7.9 all_to_all.71
  231.6 105.3 %all-gather.3 = s16[8,1024,1024]{2,1,0:T(8,128)(2,1)} all-gather(s16[8,256,1024]{2,1,0:T(8,128)(2,1)} %all_to_all.71), channel_id=1, replica_groups=mesh['row'=4,'col'=4,'pt'=2] {'row'}, dimensions={1}, use_global_device_ids=true | all-gather | bytes 20971520 | tf_op jit(solution)/shard_map/all_gather | solution.py:212
  336.9 16.5 %fusion.14 = f32[8,256,1024]{2,1,0:T(8,128)} fusion(s16[8,1024,1024]{2,1,0:T(8,128)(2,1)} %all-gather.3, f32[8,256,1024]{2,1,0:T(8,128)} %reshape.16), kind=kOutput, calls=%fused_computation.16 | convolution fusion | flops 4334813184 | bytes 33554432 | tf_op jit(solution)/shard_map/bik,bkj->bij/dot_general | solution.py:76
  353.5 17.6 %fusion.12 = f32[8,256,1024]{2,1,0:T(8,128)} fusion(s16[8,1024,1024]{2,1,0:T(8,128)(2,1)} %all-gather.3, f32[8,256,1024]{2,1,0:T(8,128)} %reshape.16), kind=kOutput, calls=%fused_computation.15 | convolution fusion | flops 4339007488 | bytes 33554432 | tf_op jit(solution)/shard_map/bik,bkj->bij/dot_general | solution.py:76
  371.0 18.3 %fusion.20 = f32[8,256,1024]{2,1,0:T(8,128)} fusion(s16[8,1024,1024]{2,1,0:T(8,128)(2,1)} %all-gather.3, f32[8,256,1024]{2,1,0:T(8,128)} %reshape.16), kind=kOutput, calls=%fused_computation.23 | convolution fusion | flops 4355784704 | bytes 33554432 | tf_op jit(solution)/shard_map/bik,bkj->bij/dot_general | solution.py:76
  389.3 25.6 %subtract_convert_fusion.5 = s16[8,256,1024]{2,1,0:T(8,128)(2,1)} fusion(f32[8,256,1024]{2,1,0:T(8,128)} %fusion.20, f32[8,256,1024]{2,1,0:T(8,128)} %fusion.12, f32[8,256,1024]{2,1,0:T(8,128)} %fusion.14, s16[8,1024,1024]{2,1,0:T(8,128)(2,1)} %all-gather.3, f32[8,256,1024]{2,1,0:T(8,128)} %reshape.16), kind=kOutput, calls=%fused_computation.59 | convolution fusion | flops 4389339136 | bytes 54525952 | tf_op jit(solution)/shard_map/bik,bkj->bij/dot_general | solution.py:76
  414.9 7.3 copy.76
  427.4 94.0 %all-to-all-done.2 = s16[8,256,1024]{1,0,2:T(8,128)(2,1)} async-done(((s16[8,256,1024]{1,0,2:T(8,128)(2,1)}), s16[8,256,1024]{1,0,2:T(8,128)(2,1)}, u32[]{:S(2)}, u32[]{:S(2)}) %all-to-all-start.2) | async-done | bytes 4194336 | tf_op jit(solution)/shard_map/all_to_all | solution.py:222
  527.9 10.5 copy.77
  545.6 8.1 subtract_convert_fusion.4
  553.7 92.9 %all-gather.4 = s16[64,256,256]{2,0,1:T(8,128)(2,1)S(1)} all-gather(s16[32,256,256]{2,0,1:T(8,128)(2,1)} %subtract_convert_fusion.4), channel_id=1, replica_groups=mesh['row'=4,'col'=4,'pt'=2] {'pt'}, dimensions={0}, use_global_device_ids=true | all-gather | bytes 12582912 | tf_op jit(solution)/shard_map/all_gather | solution.py:239
  655.7 10.0 subtract_convert_fusion.3
  681.5 8.5 subtract_convert_fusion.2
  696.6 70.7 %all-to-all-done.3 = s16[32,256,256]{2,1,0:T(8,128)(2,1)} async-done(((s16[32,256,256]{2,1,0:T(8,128)(2,1)}), s16[32,256,256]{2,1,0:T(8,128)(2,1)}, u32[]{:S(2)}, u32[]{:S(2)}) %all-to-all-start.3) | async-done | bytes 4194336 | tf_op jit(solution)/shard_map/all_to_all | solution.py:213
  779.2 12.0 copy.110
  791.2 10.8 reshape.18
  802.1 63.1 %all-to-all-done.4 = s16[32,256,256]{2,1,0:T(8,128)(2,1)} async-done(((s16[32,256,256]{2,1,0:T(8,128)(2,1)}), s16[32,256,256]{2,1,0:T(8,128)(2,1)}, u32[]{:S(2)}, u32[]{:S(2)}) %all-to-all-start.4) | async-done | bytes 4194336 | tf_op jit(solution)/shard_map/all_to_all | solution.py:209
  865.1 7.4 copy.112
  872.6 7.9 all_to_all.77
  880.5 104.5 %all-gather.5 = s16[8,1024,1024]{2,1,0:T(8,128)(2,1)} all-gather(s16[8,256,1024]{2,1,0:T(8,128)(2,1)} %all_to_all.77), channel_id=1, replica_groups=mesh['row'=4,'col'=4,'pt'=2] {'row'}, dimensions={1}, use_global_device_ids=true | all-gather | bytes 20971520 | tf_op jit(solution)/shard_map/all_gather | solution.py:212
  985.0 16.5 %fusion.10 = f32[8,256,1024]{2,1,0:T(8,128)} fusion(s16[8,1024,1024]{2,1,0:T(8,128)(2,1)} %all-gather.5, f32[8,256,1024]{2,1,0:T(8,128)} %reshape.18), kind=kOutput, calls=%fused_computation.14 | convolution fusion | flops 4334813184 | bytes 33554432 | tf_op jit(solution)/shard_map/bik,bkj->bij/dot_general | solution.py:76
  1001.6 17.6 %fusion.8 = f32[8,256,1024]{2,1,0:T(8,128)} fusion(s16[8,1024,1024]{2,1,0:T(8,128)(2,1)} %all-gather.5, f32[8,256,1024]{2,1,0:T(8,128)} %reshape.18), kind=kOutput, calls=%fused_computation.13 | convolution fusion | flops 4339007488 | bytes 33554432 | tf_op jit(solution)/shard_map/bik,bkj->bij/dot_general | solution.py:76
  1019.1 18.3 %fusion.16 = f32[8,256,1024]{2,1,0:T(8,128)} fusion(s16[8,1024,1024]{2,1,0:T(8,128)(2,1)} %all-gather.5, f32[8,256,1024]{2,1,0:T(8,128)} %reshape.18), kind=kOutput, calls=%fused_computation.21 | convolution fusion | flops 4355784704 | bytes 33554432 | tf_op jit(solution)/shard_map/bik,bkj->bij/dot_general | solution.py:76
  1037.4 25.6 %subtract_convert_fusion = s16[8,256,1024]{2,1,0:T(8,128)(2,1)} fusion(f32[8,256,1024]{2,1,0:T(8,128)} %fusion.16, f32[8,256,1024]{2,1,0:T(8,128)} %fusion.8, f32[8,256,1024]{2,1,0:T(8,128)} %fusion.10, s16[8,1024,1024]{2,1,0:T(8,128)(2,1)} %all-gather.5, f32[8,256,1024]{2,1,0:T(8,128)} %reshape.18), kind=kOutput, calls=%fused_computation.52 | convolution fusion | flops 4389339136 | bytes 54525952 | tf_op jit(solution)/shard_map/bik,bkj->bij/dot_general | solution.py:76
  1070.2 99.7 %all_to_all.90 = s16[8,256,1024]{1,0,2:T(8,128)(2,1)} all-to-all(s16[8,256,1024]{1,0,2:T(8,128)(2,1)} %copy.84), channel_id=1, replica_groups=mesh['row'=4,'col'=4,'pt'=2] {'col'}, dimensions={2} | all-to-all | bytes 8388608 | tf_op jit(solution)/shard_map/all_to_all | solution.py:222
  1169.9 7.9 copy.86
  1182.3 48.6 %all_to_all.91 = s16[32,256,256]{2,0,1:T(8,128)(2,1)S(1)} all-to-all(s16[32,256,256]{2,0,1:T(8,128)(2,1)S(1)} %copy.87), channel_id=1, replica_groups=mesh['row'=4,'col'=4,'pt'=2] {'pt'}, dimensions={1} | all-to-all | bytes 8388608 | tf_op jit(solution)/shard_map/all_to_all | solution.py:251
  (70 shorter events, 155.2 us)
Async XLA Ops:
  0.0 5.5 copy-start.3
  0.0 6.8 copy-start.2
  6.8 1.4 copy-start.11
  19.6 98.6 %all-to-all-start = ((s16[32,256,256]{2,1,0:T(8,128)(2,1)}), s16[32,256,256]{2,1,0:T(8,128)(2,1)}, u32[]{:S(2)}, u32[]{:S(2)}) async-start(s16[32,256,256]{2,1,0:T(8,128)(2,1)} %copy.69), calls=%async_computation | async-start | bytes 8388608 | tf_op jit(solution)/shard_map/all_to_all | solution.py:213
  118.2 98.0 %all-to-all-start.1 = ((s16[32,256,256]{2,1,0:T(8,128)(2,1)}), s16[32,256,256]{2,1,0:T(8,128)(2,1)}, u32[]{:S(2)}, u32[]{:S(2)}) async-start(s16[32,256,256]{2,1,0:T(8,128)(2,1)} %copy.74), calls=%async_computation.1 | async-start | bytes 8388608 | tf_op jit(solution)/shard_map/all_to_all | solution.py:209
  414.9 12.5 copy-start.1
  414.9 12.5 copy-start.4
  422.2 99.2 %all-to-all-start.2 = ((s16[8,256,1024]{1,0,2:T(8,128)(2,1)}), s16[8,256,1024]{1,0,2:T(8,128)(2,1)}, u32[]{:S(2)}, u32[]{:S(2)}) async-start(s16[8,256,1024]{1,0,2:T(8,128)(2,1)} %copy.76), calls=%async_computation.2 | async-start | bytes 8388608 | tf_op jit(solution)/shard_map/all_to_all | solution.py:222
  538.4 4.5 copy-start.8
  542.8 1.3 copy-start.7
  544.1 1.5 copy-start.10
  646.5 9.1 copy-start
  669.9 97.4 %all-to-all-start.3 = ((s16[32,256,256]{2,1,0:T(8,128)(2,1)}), s16[32,256,256]{2,1,0:T(8,128)(2,1)}, u32[]{:S(2)}, u32[]{:S(2)}) async-start(s16[32,256,256]{2,1,0:T(8,128)(2,1)} %copy.78), calls=%async_computation.3 | async-start | bytes 8388608 | tf_op jit(solution)/shard_map/all_to_all | solution.py:213
  675.0 4.3 slice-start
  678.0 2.2 slice-start.1
  767.3 97.8 %all-to-all-start.4 = ((s16[32,256,256]{2,1,0:T(8,128)(2,1)}), s16[32,256,256]{2,1,0:T(8,128)(2,1)}, u32[]{:S(2)}, u32[]{:S(2)}) async-start(s16[32,256,256]{2,1,0:T(8,128)(2,1)} %copy.82), calls=%async_computation.4 | async-start | bytes 8388608 | tf_op jit(solution)/shard_map/all_to_all | solution.py:209
  1239.6 2.2 copy-start.5
  1241.7 1.0 copy-start.6
  1242.7 1.5 copy-start.9
where the time goes:
time: 1270 us; the launch traced here: 1260 us
  blocking collectives  451 us (36%)
  waiting for transfers between devices  365 us (29%)
  matrix products  221 us (17%)
  local copies, waits for them, and re-layouts  148 us (12%)
  other arithmetic  45.2 us (4%)
  starting transfers between devices  25.7 us (2%)
    all_gather x2, blocking collectives, column_pointwise(): right_points = lax.all_gather(right_points, 'row', axis=1, tiled=True)  210 us
    dot_general x8, matrix products, batched_product(): jnp.einsum('bik,bkj->bij', left_part, right_part, preferred_element_type=...  156 us
    all_to_all x2, waiting for transfers between devices, column_pointwise(): lax.all_to_all(left_values.astype(jnp.int16), 'col', split_axis=0, concat...  145 us
    all_to_all x2, waiting for transfers between devices, column_pointwise(): lax.all_to_all(right_values.astype(jnp.int16), 'col', split_axis=0, conca...  126 us
    all_to_all x1, blocking collectives, column_pointwise(): lax.all_to_all(product_values.astype(jnp.int16), 'col', split_axis=2, con...  99.7 us
    all_to_all x1, waiting for transfers between devices, column_pointwise(): lax.all_to_all(product_values.astype(jnp.int16), 'col', split_axis=2, con...  94 us
    all_gather x1, blocking collectives, pair_local(): both_products = lax.all_gather(own_product, 'pt', axis=0, tiled=True)  92.9 us
    dot_general x18, matrix products, product_of(): jnp.einsum('ts,sab->tab', left_part, right_part, preferred_element_type=j...  65.3 us
  transfers between devices with their start and end apart: 5, of which 5 were waited for; matrix products, arithmetic and copies ran while one was open for 8% of the time, Pallas kernels for 0%

commit v1 on v0

--- a/solution.py
+++ b/solution.py
@@ -1,7 +1,11 @@
+import functools
+
 import jax
 import jax.numpy as jnp
 import numpy as np
 from jax import lax
+from jax.experimental import pallas as pl
+from jax.experimental.pallas import tpu as pltpu
 from jax.sharding import PartitionSpec as P
 
 DEG = 16
@@ -173,92 +177,539 @@
     return values - 12289.0 * jnp.round(values * (1.0 / 12289.0))
 
 
-def centred_digits(values):
-    high_digit = jnp.round(values * (1.0 / 128.0))
-    return high_digit.astype(jnp.bfloat16), (values - 128.0 * high_digit).astype(jnp.bfloat16)
-
-
-def combine_centred(high_high, middle, low_low):
-    upper_part = reduce_centred(reduce_centred(high_high) * 128.0 + middle)
-    return reduce_centred(upper_part * 128.0 + low_low)
-
-
 def table_digits(matrix_table):
     centred = np.where(matrix_table > modulus // 2, matrix_table - modulus, matrix_table)
     high_digit = np.round(centred / 128.0)
     return high_digit, centred - 128.0 * high_digit
 
 
-def centred_transform(table_high, table_low, coefs):
-    data_high, data_low = centred_digits(coefs.astype(jnp.float32))
-    table_high = jnp.asarray(table_high, dtype=jnp.bfloat16)
-    table_low = jnp.asarray(table_low, dtype=jnp.bfloat16)
-
-    def product_of(left_part, right_part):
-        return jnp.einsum("ts,sab->tab", left_part, right_part, preferred_element_type=jnp.float32)
-
-    middle = product_of(
-        jnp.concatenate([table_high, table_low], 1), jnp.concatenate([data_low, data_high], 0)
-    )
-    return combine_centred(
-        product_of(table_high, data_high), middle, product_of(table_low, data_low)
-    )
-
-
-def column_pointwise(left_values, right_values):
-    right_points = lax.all_to_all(
-        right_values.astype(jnp.int16), "col", split_axis=0, concat_axis=2, tiled=True
-    )
-    right_points = lax.all_gather(right_points, "row", axis=1, tiled=True)
-    left_points = lax.all_to_all(
-        left_values.astype(jnp.int16), "col", split_axis=0, concat_axis=2, tiled=True
-    )
-    left_high, left_low = centred_digits(left_points.astype(jnp.float32))
-    right_high, right_low = centred_digits(right_points.astype(jnp.float32))
-    middle = batched_product(left_high, right_low) + batched_product(left_low, right_high)
-    product_values = combine_centred(
-        batched_product(left_high, right_high), middle, batched_product(left_low, right_low)
-    )
-    return lax.all_to_all(
-        product_values.astype(jnp.int16), "col", split_axis=2, concat_axis=0, tiled=True
-    )
-
-
-def pair_local(first_factors, second_factors):
-    forward_one = table_digits(make_table(2 * DEG, 2 * DEG, DEG, False))
-    inverse_one = table_digits(make_table(2 * DEG, 2 * DEG, 2 * DEG, True))
-    forward_two = table_digits(make_table(4 * DEG, 4 * DEG, 2 * DEG, False))
-    inverse_two = table_digits(make_table(4 * DEG, 3 * DEG - 3, 4 * DEG, True))
-    half_points = 2 * DEG
-    place = lax.axis_index("pt")
-    products = column_pointwise(
-        centred_transform(*forward_one, centre(first_factors)),
-        centred_transform(*forward_one, centre(second_factors)),
-    )
-    own_product = centred_transform(*inverse_one, products).astype(jnp.int16)
-    both_products = lax.all_gather(own_product, "pt", axis=0, tiled=True)
-    first_product = both_products[: 2 * DEG]
-    shifted = both_products[3 * DEG :]
-    own_tables = [
-        lax.dynamic_slice_in_dim(
-            jnp.asarray(digit, dtype=jnp.bfloat16), place * half_points, half_points, 0
-        )
-        for digit in forward_two
-    ]
-    upper_values = centred_transform(*own_tables, first_product)
-    lower_values = centred_transform(*[digit[:, :DEG] for digit in own_tables], shifted)
-    products_two = column_pointwise(upper_values, lower_values)
-    all_points = lax.all_to_all(products_two, "pt", split_axis=1, concat_axis=0, tiled=True)
-    result = centred_transform(*inverse_two, all_points)
-    return jnp.where(result < 0.0, result + 12289.0, result) / 12289.0
-
-
 def centre(values):
     return jnp.where(values > modulus // 2, values - modulus, values)
+
+
+MESH = pl.DeviceIdType.MESH
+sub_rows = 8
+chunk_count = 4
+vmem_limit = 67_000_000
+
+
+def spread_table(matrix_table):
+    shifted_table = matrix_table * 128 % modulus
+    parts = [table_digits(matrix_table), table_digits(shifted_table)]
+    base = np.concatenate(
+        [128.0 * parts[0][0], 128.0 * parts[1][0], parts[0][1], parts[1][1]], axis=1
+    )
+    slots = matrix_table.shape[1]
+    weights = np.concatenate([np.full(slots, 65.0), np.full(slots, 97.0)] * 2)
+    if np.max(np.abs(base) @ weights) >= 2.0**24:
+        raise ValueError("inexact sums")
+    return jnp.asarray(np.kron(base, np.eye(sub_rows)), dtype=jnp.bfloat16)
+
+
+def low_and_high(values):
+    high_digit = jnp.round(values * (1.0 / 128.0))
+    return values - 128.0 * high_digit, high_digit
+
+
+def spread_dot(table_value, values):
+    slots, rows, columns = values.shape
+    low, high = (
+        digit.reshape(slots * rows, columns).astype(jnp.bfloat16) for digit in low_and_high(values)
+    )
+    result = jnp.dot(
+        table_value,
+        jnp.concatenate([low, high, low, high], axis=0),
+        preferred_element_type=jnp.float32,
+    )
+    return result.reshape(-1, rows, columns)
+
+
+def as_float(values):
+    return values.astype(jnp.int32).astype(jnp.float32)
+
+
+def as_short(values):
+    return values.astype(jnp.int32).astype(jnp.int16)
+
+
+def transform_group(table_ref, source_ref, block, start):
+    values = as_float(source_ref[block, :, pl.ds(start, 2 * sub_rows), :])
+    table_value = table_ref[...]
+    return jnp.concatenate(
+        [
+            reduce_centred(spread_dot(table_value, values[:, :sub_rows])),
+            reduce_centred(spread_dot(table_value, values[:, sub_rows:])),
+        ],
+        axis=1,
+    )
+
+
+def transform_left(table_ref, source_ref, block, digits_ref):
+    rows, columns = source_ref.shape[2:]
+
+    def group(index, carry):
+        start = pl.multiple_of(index * 2 * sub_rows, 2 * sub_rows)
+        values = transform_group(table_ref, source_ref, block, start)
+        low, high = low_and_high(values)
+        shifted_low = jnp.round(values * (-1.0 / 96.0))
+        shifted_high = values + 96.0 * shifted_low
+        top, bottom = pl.ds(start, 2 * sub_rows), pl.ds(rows + start, 2 * sub_rows)
+        digits_ref[:, top, :columns] = shifted_high.astype(jnp.bfloat16)
+        digits_ref[:, top, columns:] = high.astype(jnp.bfloat16)
+        digits_ref[:, bottom, :columns] = shifted_low.astype(jnp.bfloat16)
+        digits_ref[:, bottom, columns:] = low.astype(jnp.bfloat16)
+        return carry
+
+    lax.fori_loop(0, rows // (2 * sub_rows), group, 0)
+
+
+def transform_right(table_ref, source_ref, block, digits_ref):
+    rows = source_ref.shape[2]
+
+    def group(index, carry):
+        start = pl.multiple_of(index * 2 * sub_rows, 2 * sub_rows)
+        values = transform_group(table_ref, source_ref, block, start)
+        low, high = low_and_high(values)
+        digits_ref[:, pl.ds(start, 2 * sub_rows), :] = high.astype(jnp.bfloat16)
+        digits_ref[:, pl.ds(rows + start, 2 * sub_rows), :] = low.astype(jnp.bfloat16)
+        return carry
+
+    lax.fori_loop(0, rows // (2 * sub_rows), group, 0)
+
+
+def multiply_points(left_ref, right_ref, totals_ref, first):
+    def point(index, carry):
+        product = jnp.dot(left_ref[index], right_ref[index], preferred_element_type=jnp.float32)
+
+        @pl.when(first)
+        def _():
+            totals_ref[index] = product
+
+        @pl.when(jnp.logical_not(first))
+        def _():
+            totals_ref[index] += product
+
+        return carry
+
+    lax.fori_loop(0, left_ref.shape[0], point, 0)
+
+
+def folded(totals_ref, start, rows):
+    high = totals_ref[:, pl.ds(start, rows), :]
+    low = totals_ref[:, pl.ds(totals_ref.shape[1] // 2 + start, rows), :]
+    values = reduce_centred(reduce_centred(high) * 128.0 + low)
+    half = values.shape[0] // 2
+    return values[:half] + values[half:], values[:half] - values[half:]
+
+
+def remote(source, target, send, receive, **place):
+    return pltpu.make_async_remote_copy(
+        src_ref=source,
+        dst_ref=target,
+        send_sem=send,
+        recv_sem=receive,
+        device_id=place,
+        device_id_type=MESH,
+    )
+
+
+class Line:
+    def __init__(self, axis, size, buffer, slots, send, receive):
+        self.axis, self.size, self.buffer = axis, size, buffer
+        self.place = lax.axis_index(axis)
+        self.slots = slots
+        self.send, self.receive = send, receive
+        self.rows = buffer.shape[2] // chunk_count
+
+    def copy(self, direction, step, chunk, block):
+        rows = pl.ds(pl.multiple_of(chunk * self.rows, self.rows), self.rows)
+        part = self.buffer.at[block, pl.ds(0, self.slots), rows, :]
+        target = self.place + (1 if direction else -1)
+        return remote(
+            part,
+            part,
+            self.send.at[direction, step, chunk],
+            self.receive.at[direction, step, chunk],
+            **{self.axis: target},
+        )
+
+    def sends(self, step, act):
+        pl.when((self.place > 0) & (self.place + step < self.size))(
+            lambda: act(0, self.place + step)
+        )
+        pl.when((self.place < self.size - 1) & (self.place - step >= 0))(
+            lambda: act(1, self.place - step)
+        )
+
+    def start(self, chunk):
+        self.sends(0, lambda direction, block: self.copy(direction, 0, chunk, block).start())
+
+    def tick(self, step, chunk):
+        def arrive(direction, block):
+            self.copy(direction, step, chunk, block).wait_recv()
+
+        pl.when(self.place + step + 1 < self.size)(lambda: arrive(0, self.place + step + 1))
+        pl.when(self.place - step - 1 >= 0)(lambda: arrive(1, self.place - step - 1))
+
+        @pl.when(step + 1 < self.size - 1)
+        def _():
+            self.sends(
+                step + 1,
+                lambda direction, block: self.copy(direction, step + 1, chunk, block).start(),
+            )
+
+    def finish(self):
+        def one(index, carry):
+            step, chunk = index // chunk_count, index % chunk_count
+            self.sends(
+                step, lambda direction, block: self.copy(direction, step, chunk, block).wait_send()
+            )
+            return carry
+
+        lax.fori_loop(0, (self.size - 1) * chunk_count, one, 0)
+
+    def block_at(self, position):
+        first = self.place + 1 - 2 * (self.place // (self.size - 1))
+        last = (self.size - 1) * (1 - self.place // (self.size // 2))
+        third = self.size * (self.size - 1) // 2 - self.place - first - last
+        return (
+            jnp.where(position == 0, self.place, 0)
+            + jnp.where(position == 1, first, 0)
+            + jnp.where(position == 2, third, 0)
+            + jnp.where(position == 3, last, 0)
+        )
+
+
+class Square:
+    def __init__(self, axis, buffer, slots, send, receive):
+        self.axis, self.buffer, self.slots = axis, buffer, slots
+        self.place = lax.axis_index(axis)
+        self.near = self.place + 1 - 2 * (self.place % 2)
+        self.far = (self.place + 2) % 4
+        self.send, self.receive = send, receive
+        self.rows = buffer.shape[2] // chunk_count
+
+    def copy(self, kind, chunk, sending):
+        rows = pl.ds(pl.multiple_of(chunk * self.rows, self.rows), self.rows)
+        if kind == 0:
+            block, target = (self.place if sending else self.far), self.far
+        elif kind == 1:
+            block, target = (self.place if sending else self.near), self.near
+        else:
+            block, target = (self.far if sending else (self.near + 2) % 4), self.near
+        part = self.buffer.at[block, pl.ds(0, self.slots), rows, :]
+        return remote(
+            part, part, self.send.at[kind, chunk], self.receive.at[kind, chunk], **{self.axis: target}
+        )
+
+    def start(self, chunk):
+        self.copy(0, chunk, True).start()
+        self.copy(1, chunk, True).start()
+
+    def tick(self, chunk):
+        self.copy(0, chunk, False).wait_recv()
+        self.copy(2, chunk, True).start()
+
+    def arrive(self, chunk):
+        self.copy(1, chunk, False).wait_recv()
+        self.copy(2, chunk, False).wait_recv()
+
+    def finish(self, chunk):
+        for kind in range(3):
+            self.copy(kind, chunk, True).wait_send()
+
+
+def each_chunk(act):
+    def one(chunk, carry):
+        act(chunk)
+        return carry
+
+    lax.fori_loop(0, chunk_count, one, 0)
+
+
+def greet(line, square, others=()):
+    barrier = pltpu.get_barrier_semaphore()
+
+    def signal(**place):
+        pl.semaphore_signal(barrier, inc=1, device_id=place, device_id_type=MESH)
+
+    for target in (square.near, square.far):
+        signal(**{square.axis: target})
+    for place in others:
+        signal(**place)
+    before, after = line.place > 0, line.place < line.size - 1
+    pl.when(before)(lambda: signal(**{line.axis: line.place - 1}))
+    pl.when(after)(lambda: signal(**{line.axis: line.place + 1}))
+    ends = (line.place + line.size - 1) // line.size + 1 - (line.place + 1) // line.size
+    pl.semaphore_wait(barrier, 2 + len(others) + ends)
+
+
+def pipeline(line, square, left, right, multiply):
+    each_chunk(lambda chunk: (line.tick(0, chunk), square.tick(chunk)))
+    each_chunk(square.arrive)
+    tick_count = (line.size - 2) * chunk_count
+
+    def one(index, carry):
+        pl.when(index < tick_count)(
+            lambda: line.tick(1 + index // chunk_count, index % chunk_count)
+        )
+        position = jnp.where(index < tick_count, index // 2, line.size - 1)
+        works = (index < 2 * (line.size - 1)) | (index >= tick_count)
+
+        @pl.when(works & (index % 2 == 0))
+        def _():
+            block = line.block_at(position)
+            left(block)
+            right(block)
+
+        @pl.when(works & (index % 2 == 1))
+        def _():
+            multiply(position == 0)
+
+        return carry
+
+    lax.fori_loop(0, tick_count + 2, one, 0)
+    line.finish()
+    each_chunk(square.finish)
+
+
+def product_kernel(
+    size,
+    left_hbm,
+    right_hbm,
+    forward_ref,
+    even_ref,
+    odd_ref,
+    out_ref,
+    left_ref,
+    right_ref,
+    left_digits,
+    right_digits,
+    totals,
+    line_send,
+    line_receive,
+    square_send,
+    square_receive,
+    local_sems,
+):
+    slots = left_ref.shape[1]
+    line = Line("col", size, left_ref, slots, line_send, line_receive)
+    square = Square("row", right_ref, slots, square_send, square_receive)
+    copies = (
+        pltpu.make_async_copy(left_hbm, left_ref.at[line.place], local_sems.at[0]),
+        pltpu.make_async_copy(right_hbm, right_ref.at[square.place], local_sems.at[1]),
+    )
+    for copy in copies:
+        copy.start()
+    greet(line, square)
+    for copy in copies:
+        copy.wait()
+    each_chunk(lambda chunk: (line.start(chunk), square.start(chunk)))
+    pipeline(
+        line,
+        square,
+        lambda block: transform_left(forward_ref, left_ref, block, left_digits),
+        lambda block: transform_right(forward_ref, right_ref, block, right_digits),
+        lambda first: multiply_points(left_digits, right_digits, totals, first),
+    )
+
+    def group(index, carry):
+        start = pl.multiple_of(index * 2 * sub_rows, 2 * sub_rows)
+        halves = []
+        for half in range(2):
+            sums, differences = folded(totals, start + half * sub_rows, sub_rows)
+            halves.append(
+                [
+                    reduce_centred(spread_dot(even_ref[...], sums)),
+                    reduce_centred(spread_dot(odd_ref[...], differences)),
+                ]
+            )
+        for parity in range(2):
+            values = as_short(jnp.concatenate([halves[0][parity], halves[1][parity]], axis=1))
+            for place in range(values.shape[0]):
+                out_ref[2 * place + parity, pl.ds(start, 2 * sub_rows), :] = values[place]
+        return carry
+
+    lax.fori_loop(0, out_ref.shape[1] // (2 * sub_rows), group, 0)
+
+
+def result_kernel(
+    size,
+    product_hbm,
+    upper_table,
+    lower_table,
+    even_ref,
+    odd_ref,
+    out_ref,
+    left_ref,
+    right_ref,
+    left_digits,
+    right_digits,
+    totals,
+    line_send,
+    line_receive,
+    square_send,
+    square_receive,
+    cross_send,
+    cross_receive,
+    local_sems,
+):
+    left_slots, right_slots = left_ref.shape[1] - 1, right_ref.shape[1] - 1
+    rows = left_ref.shape[2]
+    line = Line("col", size, left_ref, left_slots, line_send, line_receive)
+    square = Square("row", right_ref, right_slots, square_send, square_receive)
+    side = lax.axis_index("pt")
+    own_left = product_hbm.at[pl.ds(0, left_slots), pl.ds(0, rows), :]
+    own_right = product_hbm.at[pl.ds(right_ref.shape[1], right_slots), :, :]
+    copy_left = pltpu.make_async_copy(
+        own_left, left_ref.at[line.place, pl.ds(0, left_slots)], local_sems.at[0]
+    )
+    copy_right = pltpu.make_async_copy(
+        own_right, right_ref.at[square.place, pl.ds(0, right_slots)], local_sems.at[1]
+    )
+    pl.when(side == 0)(copy_left.start)
+    pl.when(side == 1)(copy_right.start)
+    for block in range(size):
+        left_ref[block, left_slots] = jnp.zeros(left_ref.shape[2:], left_ref.dtype)
+        right_ref[block, right_slots] = jnp.zeros(right_ref.shape[2:], right_ref.dtype)
+    greet(line, square, ({"pt": 1 - side},))
+
+    def cross_left(chunk):
+        part = pl.multiple_of(chunk * line.rows, line.rows)
+        return remote(
+            product_hbm.at[pl.ds(0, left_slots), pl.ds(rows + part, line.rows), :],
+            left_ref.at[line.place, pl.ds(0, left_slots), pl.ds(part, line.rows), :],
+            cross_send.at[chunk],
+            cross_receive.at[chunk],
+            pt=1 - side,
+        )
+
+    def cross_right(chunk):
+        part = pl.multiple_of(chunk * square.rows, square.rows)
+        return remote(
+            product_hbm.at[
+                pl.ds(right_ref.shape[1], right_slots), pl.ds(part, square.rows), :
+            ],
+            right_ref.at[square.place, pl.ds(0, right_slots), pl.ds(part, square.rows), :],
+            cross_send.at[chunk],
+            cross_receive.at[chunk],
+            pt=1 - side,
+        )
+
+    @pl.when(side == 0)
+    def _():
+        each_chunk(lambda chunk: cross_left(chunk).start())
+        copy_left.wait()
+        each_chunk(line.start)
+        each_chunk(lambda chunk: (cross_right(chunk).wait_recv(), square.start(chunk)))
+
+    @pl.when(side == 1)
+    def _():
+        each_chunk(lambda chunk: cross_right(chunk).start())
+        copy_right.wait()
+        each_chunk(square.start)
+        each_chunk(lambda chunk: (cross_left(chunk).wait_recv(), line.start(chunk)))
+
+    pipeline(
+        line,
+        square,
+        lambda block: transform_left(upper_table, left_ref, block, left_digits),
+        lambda block: transform_right(lower_table, right_ref, block, right_digits),
+        lambda first: multiply_points(left_digits, right_digits, totals, first),
+    )
+    pl.when(side == 0)(lambda: each_chunk(lambda chunk: cross_left(chunk).wait_send()))
+    pl.when(side == 1)(lambda: each_chunk(lambda chunk: cross_right(chunk).wait_send()))
+
+    def group(index, carry):
+        start = pl.multiple_of(index * sub_rows, sub_rows)
+        for parity, (table_ref, values) in enumerate(
+            zip((even_ref, odd_ref), folded(totals, start, sub_rows))
+        ):
+            result = reduce_centred(spread_dot(table_ref[...], values))
+            result = jnp.where(result < 0.0, result + 12289.0, result) * (1.0 / 12289.0)
+            for place in range(result.shape[0]):
+                out_ref[2 * place + parity, pl.ds(start, sub_rows), :] = result[place]
+        return carry
+
+    lax.fori_loop(0, out_ref.shape[1] // sub_rows, group, 0)
+
+
+def call(kernel, collective_id, arguments, tables, out_shape, out_dtype, shapes, extra=()):
+    left, right, points = shapes
+    size, rows, columns = left[0], left[2], left[3]
+    inner, width = right[2], right[3]
+    return pl.pallas_call(
+        functools.partial(kernel, size),
+        out_shape=jax.ShapeDtypeStruct(out_shape, out_dtype),
+        in_specs=[pl.BlockSpec(memory_space=pl.ANY)] * len(arguments)
+        + [pl.BlockSpec(memory_space=pltpu.VMEM)] * len(tables),
+        out_specs=pl.BlockSpec(memory_space=pltpu.VMEM),
+        scratch_shapes=[
+            pltpu.VMEM(left, jnp.int16),
+            pltpu.VMEM(right, jnp.int16),
+            pltpu.VMEM((points, 2 * rows, 2 * columns), jnp.bfloat16),
+            pltpu.VMEM((points, 2 * inner, width), jnp.bfloat16),
+            pltpu.VMEM((points, 2 * rows, width), jnp.float32),
+            pltpu.SemaphoreType.DMA((2, size - 1, chunk_count)),
+            pltpu.SemaphoreType.DMA((2, size - 1, chunk_count)),
+            pltpu.SemaphoreType.DMA((3, chunk_count)),
+            pltpu.SemaphoreType.DMA((3, chunk_count)),
+            *extra,
+            pltpu.SemaphoreType.DMA((2,)),
+        ],
+        compiler_params=pltpu.CompilerParams(
+            collective_id=collective_id, has_side_effects=True, vmem_limit_bytes=vmem_limit
+        ),
+        name=kernel.__name__,
+    )(*arguments, *tables)
+
+
+def square_local(first_factors, second_factors):
+    size = lax.axis_size("col")
+    slots, rows, columns = first_factors.shape
+    points = 2 * slots
+    inverse_one = make_table(points, points, points, True)
+    left, right = (centre(values).astype(jnp.int16) for values in (first_factors, second_factors))
+    products = call(
+        product_kernel,
+        0,
+        (left, right),
+        [
+            spread_table(make_table(points, points, slots, False)),
+            spread_table(inverse_one[0::2, :slots]),
+            spread_table(inverse_one[1::2, :slots]),
+        ],
+        (points, rows, columns),
+        jnp.int16,
+        ((size, slots, rows, columns), (size, slots, rows, columns), points),
+    )
+    last_points = 3 * slots
+    inverse_two = make_table(last_points, last_points - 3, last_points, True)
+    half = last_points // 2
+    own_rows = rows // lax.axis_size("pt")
+    return call(
+        result_kernel,
+        1,
+        (products,),
+        [
+            spread_table(make_table(last_points, last_points, points, False)),
+            spread_table(make_table(last_points, last_points, slots, False)),
+            spread_table(inverse_two[0::2, :half]),
+            spread_table(inverse_two[1::2, :half]),
+        ],
+        (last_points - 3, own_rows, columns),
+        jnp.float32,
+        ((size, points, own_rows, columns), (size, slots, rows, columns), last_points),
+        extra=(
+            pltpu.SemaphoreType.DMA((chunk_count,)),
+            pltpu.SemaphoreType.DMA((chunk_count,)),
+        ),
+    )
 
 
 def solution(mesh):
     in_specs = (P("pt", "row", "col"), P("pt", "row", "col"))
     out_specs = P(None, ("row", "pt"), "col")
-    body = pair_local if mesh.shape["pt"] == 2 else local
+    squares = mesh.shape["row"] == 4 and mesh.shape["col"] == 4 and mesh.shape["pt"] == 2
+    body = square_local if squares else local
     return jax.shard_map(body, mesh=mesh, in_specs=in_specs, out_specs=out_specs, check_vma=False)

time: 1270 us -> 394 us (0.31); the launches traced: 1260 us -> 394 us
  blocking collectives: 451 us -> 0 us
  Pallas kernels: 0 us -> 381 us
  waiting for transfers between devices: 365 us -> 0 us
  matrix products: 221 us -> 0 us
  local copies, waits for them, and re-layouts: 148 us -> 5.93 us
  other arithmetic: 45.2 us -> 6.58 us
  starting transfers between devices: 25.7 us -> 0 us
    pallas_call x0 -> x2, Pallas kernels: none -> 381 us  [call(): pl.pallas_call(functools.partial(kernel, size), out_shape=jax.ShapeDtypeS...]
    all_to_all x5 -> x0, waiting for transfers between devices: 365 us -> none  [the longest x2 145 us: column_pointwise(): lax.all_to_all(left_values.astype(jnp.int16), 'col', split_axis=0, concat...]
    all_gather x3 -> x0, blocking collectives: 303 us -> none  [the longest x2 210 us: column_pointwise(): right_points = lax.all_gather(right_points, 'row', axis=1, tiled=True)]
    dot_general x26 -> x0, matrix products: 221 us -> none  [the longest x8 156 us: batched_product(): jnp.einsum('bik,bkj->bij', left_part, right_part, preferred_element_type=...]
    all_to_all x2 -> x0, blocking collectives: 148 us -> none  [the longest x1 99.7 us: column_pointwise(): lax.all_to_all(product_values.astype(jnp.int16), 'col', split_axis=2, con...]
    convert_element_type x12 -> x0, local copies, waits for them, and re-layouts: 95.2 us -> none  [the longest x4 45.7 us: column_pointwise(): left_high, left_low = centred_digits(left_points.astype(jnp.float32))]
    all_to_all x7 -> x0, local copies, waits for them, and re-layouts: 45.5 us -> none  [the longest x4 30.7 us: column_pointwise(): lax.all_to_all(right_values.astype(jnp.int16), 'col', split_axis=0, conca...]
    convert_element_type x10 -> x1, other arithmetic: 45.2 us -> 6.58 us  [square_local(): centre(values).astype(jnp.int16)]
  transfers between devices with their start and end apart: 5 -> 0, of which waited for: 5 -> 0; matrix products, arithmetic and copies ran while one was open for 8% -> 0% of each run, Pallas kernels for 0% -> 0%
where the time goes in v1:
time: 394 us
  Pallas kernels  381 us (97%)
  other arithmetic  6.58 us (2%)
  local copies, waits for them, and re-layouts  5.93 us (2%)
    pallas_call x2, Pallas kernels, call(): pl.pallas_call(functools.partial(kernel, size), out_shape=jax.ShapeDtypeS...  381 us

profile of v1, /device:TPU:4, one launch (start us, length us, event | category | flops | bytes accessed | tf_op | source)
XLA Modules:
  0.0 393.8 jit_solution(16327629743027624207)
XLA Ops:
  0.0 6.6 %fusion = (s16[16,256,256]{2,1,0:T(8,128)(2,1)}, s16[16,256,256]{2,1,0:T(8,128)(2,1)}) fusion(s32[16,256,256]{2,1,0:T(8,128)} %param.9, s32[16,256,256]{2,1,0:T(8,128)} %param.10), kind=kLoop, calls=%fused_computation.2 | loop fusion | flops 8388608 | bytes 12582912 | tf_op jit(solution)/shard_map/convert_element_type | solution.py:672
  6.6 181.8 %product_kernel.1.product_hbm = s16[32,256,256]{2,1,0:T(8,128)(2,1)} custom-call(s16[16,256,256]{2,1,0:T(8,128)(2,1)} %get-tuple-element.5.left_hbm, s16[16,256,256]{2,1,0:T(8,128)(2,1)} %get-tuple-element.6.right_hbm, bf16[256,512]{1,0:T(8,128)(2,1)} %constant.20.clone.forward_ref, bf16[128,512]{1,0:T(8,128)(2,1)} %constant.21.clone.even_ref, ...), custom_call_target="tpu_custom_call" | custom-call | tf_op jit(solution)/shard_map/product_kernel/pallas_call | solution.py:641
  188.4 199.5 %result_kernel.1 = f32[45,128,256]{2,1,0:T(8,128)} custom-call(s16[32,256,256]{2,1,0:T(8,128)(2,1)} %product_kernel.1.product_hbm, bf16[384,1024]{1,0:T(8,128)(2,1)} %constant.23.clone.upper_table, bf16[384,512]{1,0:T(8,128)(2,1)} %constant.24.clone.lower_table, bf16[184,768]{1,0:T(8,128)(2,1)} %constant.25.clone.even_ref, ...), custom_call_target="tpu_custom_call" | custom-call | tf_op jit(solution)/shard_map/result_kernel/pallas_call | solution.py:641
  387.8 5.9 %copy.11 = f32[45,128,256]{2,1,0:T(8,128)} copy(f32[45,128,256]{2,1,0:T(8,128)} %result_kernel.1) | data formatting | bytes 11796480

commit v2 on v1

--- a/solution.py
+++ b/solution.py
@@ -244,8 +244,15 @@
     )
 
 
-def transform_left(table_ref, source_ref, block, digits_ref):
-    rows, columns = source_ref.shape[2:]
+def digit_rows(start, chunk_rows):
+    top = start // chunk_rows * (2 * chunk_rows) + start % chunk_rows
+    return pl.multiple_of(top, sub_rows), pl.multiple_of(top + chunk_rows, sub_rows)
+
+
+def transform_left(table_ref, source_ref, block, chunk, count, digits_ref):
+    columns = source_ref.shape[3]
+    chunk_rows = source_ref.shape[2] // chunk_count
+    groups = chunk_rows // (2 * sub_rows)
 
     def group(index, carry):
         start = pl.multiple_of(index * 2 * sub_rows, 2 * sub_rows)
@@ -253,14 +260,17 @@
         low, high = low_and_high(values)
         shifted_low = jnp.round(values * (-1.0 / 96.0))
         shifted_high = values + 96.0 * shifted_low
-        top, bottom = pl.ds(start, 2 * sub_rows), pl.ds(rows + start, 2 * sub_rows)
+        top, bottom = (
+            pl.ds(pl.multiple_of(place, 2 * sub_rows), 2 * sub_rows)
+            for place in digit_rows(start, chunk_rows)
+        )
         digits_ref[:, top, :columns] = shifted_high.astype(jnp.bfloat16)
         digits_ref[:, top, columns:] = high.astype(jnp.bfloat16)
         digits_ref[:, bottom, :columns] = shifted_low.astype(jnp.bfloat16)
         digits_ref[:, bottom, columns:] = low.astype(jnp.bfloat16)
         return carry
 
-    lax.fori_loop(0, rows // (2 * sub_rows), group, 0)
+    lax.fori_loop(chunk * groups, (chunk + count) * groups, group, 0)
 
 
 def transform_right(table_ref, source_ref, block, digits_ref):
@@ -277,26 +287,32 @@
     lax.fori_loop(0, rows // (2 * sub_rows), group, 0)
 
 
-def multiply_points(left_ref, right_ref, totals_ref, first):
+point_unroll = 4
+
+
+def multiply_points(left_ref, right_ref, totals_ref, first, chunk=None):
+    if chunk is None:
+        rows = slice(None)
+    else:
+        count = left_ref.shape[1] // chunk_count
+        rows = pl.ds(pl.multiple_of(chunk * count, count), count)
+
     def point(index, carry):
-        product = jnp.dot(left_ref[index], right_ref[index], preferred_element_type=jnp.float32)
-
-        @pl.when(first)
-        def _():
-            totals_ref[index] = product
-
-        @pl.when(jnp.logical_not(first))
-        def _():
-            totals_ref[index] += product
-
+        for place in range(point_unroll):
+            at = index * point_unroll + place
+            product = jnp.dot(
+                left_ref[at, rows, :], right_ref[at], preferred_element_type=jnp.float32
+            )
+            totals_ref[at, rows, :] = product if first else totals_ref[at, rows, :] + product
         return carry
 
-    lax.fori_loop(0, left_ref.shape[0], point, 0)
-
-
-def folded(totals_ref, start, rows):
-    high = totals_ref[:, pl.ds(start, rows), :]
-    low = totals_ref[:, pl.ds(totals_ref.shape[1] // 2 + start, rows), :]
+    lax.fori_loop(0, left_ref.shape[0] // point_unroll, point, 0)
+
+
+def folded(totals_ref, start, rows, chunk_rows):
+    top, bottom = digit_rows(start, chunk_rows)
+    high = totals_ref[:, pl.ds(top, rows), :]
+    low = totals_ref[:, pl.ds(bottom, rows), :]
     values = reduce_centred(reduce_centred(high) * 128.0 + low)
     half = values.shape[0] // 2
     return values[:half] + values[half:], values[:half] - values[half:]
@@ -444,31 +460,35 @@
     pl.semaphore_wait(barrier, 2 + len(others) + ends)
 
 
-def pipeline(line, square, left, right, multiply):
-    each_chunk(lambda chunk: (line.tick(0, chunk), square.tick(chunk)))
+def pipeline(line, square, left, right, multiply, finish):
+    def first(chunk):
+        line.tick(0, chunk)
+        square.tick(chunk)
+        left(line.block_at(0), chunk, 1)
+
+    each_chunk(first)
     each_chunk(square.arrive)
-    tick_count = (line.size - 2) * chunk_count
-
-    def one(index, carry):
-        pl.when(index < tick_count)(
-            lambda: line.tick(1 + index // chunk_count, index % chunk_count)
-        )
-        position = jnp.where(index < tick_count, index // 2, line.size - 1)
-        works = (index < 2 * (line.size - 1)) | (index >= tick_count)
-
-        @pl.when(works & (index % 2 == 0))
-        def _():
-            block = line.block_at(position)
-            left(block)
-            right(block)
-
-        @pl.when(works & (index % 2 == 1))
-        def _():
-            multiply(position == 0)
-
-        return carry
-
-    lax.fori_loop(0, tick_count + 2, one, 0)
+    line.tick(1, 0)
+    right(line.block_at(0))
+    multiply(True)
+    line.tick(1, 1)
+    left(line.block_at(1), 0, chunk_count)
+    right(line.block_at(1))
+    line.tick(1, 2)
+    multiply(False)
+    line.tick(1, 3)
+    left(line.block_at(2), 0, chunk_count)
+    right(line.block_at(2))
+    multiply(False)
+    right(line.block_at(3))
+
+    def last(chunk):
+        line.tick(line.size - 2, chunk)
+        left(line.block_at(line.size - 1), chunk, 1)
+        multiply(False, chunk)
+        finish(chunk)
+
+    each_chunk(last)
     line.finish()
     each_chunk(square.finish)
 
@@ -505,32 +525,37 @@
     for copy in copies:
         copy.wait()
     each_chunk(lambda chunk: (line.start(chunk), square.start(chunk)))
+    chunk_rows = line.rows
+    groups = chunk_rows // (2 * sub_rows)
+
+    def finish(chunk):
+        def group(index, carry):
+            start = pl.multiple_of(index * 2 * sub_rows, 2 * sub_rows)
+            halves = []
+            for half in range(2):
+                sums, differences = folded(totals, start + half * sub_rows, sub_rows, chunk_rows)
+                halves.append(
+                    [
+                        reduce_centred(spread_dot(even_ref[...], sums)),
+                        reduce_centred(spread_dot(odd_ref[...], differences)),
+                    ]
+                )
+            for parity in range(2):
+                values = as_short(jnp.concatenate([halves[0][parity], halves[1][parity]], axis=1))
+                for place in range(values.shape[0]):
+                    out_ref[2 * place + parity, pl.ds(start, 2 * sub_rows), :] = values[place]
+            return carry
+
+        lax.fori_loop(chunk * groups, (chunk + 1) * groups, group, 0)
+
     pipeline(
         line,
         square,
-        lambda block: transform_left(forward_ref, left_ref, block, left_digits),
+        lambda *place: transform_left(forward_ref, left_ref, *place, left_digits),
         lambda block: transform_right(forward_ref, right_ref, block, right_digits),
-        lambda first: multiply_points(left_digits, right_digits, totals, first),
-    )
-
-    def group(index, carry):
-        start = pl.multiple_of(index * 2 * sub_rows, 2 * sub_rows)
-        halves = []
-        for half in range(2):
-            sums, differences = folded(totals, start + half * sub_rows, sub_rows)
-            halves.append(
-                [
-                    reduce_centred(spread_dot(even_ref[...], sums)),
-                    reduce_centred(spread_dot(odd_ref[...], differences)),
-                ]
-            )
-        for parity in range(2):
-            values = as_short(jnp.concatenate([halves[0][parity], halves[1][parity]], axis=1))
-            for place in range(values.shape[0]):
-                out_ref[2 * place + parity, pl.ds(start, 2 * sub_rows), :] = values[place]
-        return carry
-
-    lax.fori_loop(0, out_ref.shape[1] // (2 * sub_rows), group, 0)
+        lambda *place: multiply_points(left_digits, right_digits, totals, *place),
+        finish,
+    )
 
 
 def result_kernel(
@@ -610,28 +635,33 @@
         each_chunk(square.start)
         each_chunk(lambda chunk: (cross_left(chunk).wait_recv(), line.start(chunk)))
 
+    chunk_rows = line.rows
+    groups = chunk_rows // sub_rows
+
+    def finish(chunk):
+        def group(index, carry):
+            start = pl.multiple_of(index * sub_rows, sub_rows)
+            for parity, (table_ref, values) in enumerate(
+                zip((even_ref, odd_ref), folded(totals, start, sub_rows, chunk_rows))
+            ):
+                result = reduce_centred(spread_dot(table_ref[...], values))
+                result = jnp.where(result < 0.0, result + 12289.0, result) * (1.0 / 12289.0)
+                for place in range(result.shape[0]):
+                    out_ref[2 * place + parity, pl.ds(start, sub_rows), :] = result[place]
+            return carry
+
+        lax.fori_loop(chunk * groups, (chunk + 1) * groups, group, 0)
+
     pipeline(
         line,
         square,
-        lambda block: transform_left(upper_table, left_ref, block, left_digits),
+        lambda *place: transform_left(upper_table, left_ref, *place, left_digits),
         lambda block: transform_right(lower_table, right_ref, block, right_digits),
-        lambda first: multiply_points(left_digits, right_digits, totals, first),
+        lambda *place: multiply_points(left_digits, right_digits, totals, *place),
+        finish,
     )
     pl.when(side == 0)(lambda: each_chunk(lambda chunk: cross_left(chunk).wait_send()))
     pl.when(side == 1)(lambda: each_chunk(lambda chunk: cross_right(chunk).wait_send()))
-
-    def group(index, carry):
-        start = pl.multiple_of(index * sub_rows, sub_rows)
-        for parity, (table_ref, values) in enumerate(
-            zip((even_ref, odd_ref), folded(totals, start, sub_rows))
-        ):
-            result = reduce_centred(spread_dot(table_ref[...], values))
-            result = jnp.where(result < 0.0, result + 12289.0, result) * (1.0 / 12289.0)
-            for place in range(result.shape[0]):
-                out_ref[2 * place + parity, pl.ds(start, sub_rows), :] = result[place]
-        return carry
-
-    lax.fori_loop(0, out_ref.shape[1] // sub_rows, group, 0)
 
 
 def call(kernel, collective_id, arguments, tables, out_shape, out_dtype, shapes, extra=()):

time: 394 us -> 343 us (0.87)
  Pallas kernels: 381 us -> 331 us
    pallas_call x2, Pallas kernels: 381 us -> 331 us  [call(): pl.pallas_call(functools.partial(kernel, size), out_shape=jax.ShapeDtypeS...]
where the time goes in v2:
time: 343 us
  Pallas kernels  331 us (97%)
  other arithmetic  6.58 us (2%)
  local copies, waits for them, and re-layouts  5.93 us (2%)
    pallas_call x2, Pallas kernels, call(): pl.pallas_call(functools.partial(kernel, size), out_shape=jax.ShapeDtypeS...  331 us

profile of v2, /device:TPU:4, one launch (start us, length us, event | category | flops | bytes accessed | tf_op | source)
XLA Modules:
  0.0 343.2 jit_solution(12522625222948616054)
XLA Ops:
  0.0 6.6 %fusion = (s16[16,256,256]{2,1,0:T(8,128)(2,1)}, s16[16,256,256]{2,1,0:T(8,128)(2,1)}) fusion(s32[16,256,256]{2,1,0:T(8,128)} %param.9, s32[16,256,256]{2,1,0:T(8,128)} %param.10), kind=kLoop, calls=%fused_computation.2 | loop fusion | flops 8388608 | bytes 12582912 | tf_op jit(solution)/shard_map/convert_element_type | solution.py:702
  6.6 156.6 %product_kernel.1.product_hbm = s16[32,256,256]{2,1,0:T(8,128)(2,1)} custom-call(s16[16,256,256]{2,1,0:T(8,128)(2,1)} %get-tuple-element.5.left_hbm, s16[16,256,256]{2,1,0:T(8,128)(2,1)} %get-tuple-element.6.right_hbm, bf16[256,512]{1,0:T(8,128)(2,1)} %constant.20.clone.forward_ref, bf16[128,512]{1,0:T(8,128)(2,1)} %constant.21.clone.even_ref, ...), custom_call_target="tpu_custom_call" | custom-call | tf_op jit(solution)/shard_map/product_kernel/pallas_call | solution.py:671
  163.2 174.1 %result_kernel.1 = f32[45,128,256]{2,1,0:T(8,128)} custom-call(s16[32,256,256]{2,1,0:T(8,128)(2,1)} %product_kernel.1.product_hbm, bf16[384,1024]{1,0:T(8,128)(2,1)} %constant.23.clone.upper_table, bf16[384,512]{1,0:T(8,128)(2,1)} %constant.24.clone.lower_table, bf16[184,768]{1,0:T(8,128)(2,1)} %constant.25.clone.even_ref, ...), custom_call_target="tpu_custom_call" | custom-call | tf_op jit(solution)/shard_map/result_kernel/pallas_call | solution.py:671
  337.2 5.9 %copy.11 = f32[45,128,256]{2,1,0:T(8,128)} copy(f32[45,128,256]{2,1,0:T(8,128)} %result_kernel.1) | data formatting | bytes 11796480

commit v3 on v2

--- a/solution.py
+++ b/solution.py
@@ -211,17 +211,24 @@
     return values - 128.0 * high_digit, high_digit
 
 
-def spread_dot(table_value, values):
-    slots, rows, columns = values.shape
-    low, high = (
-        digit.reshape(slots * rows, columns).astype(jnp.bfloat16) for digit in low_and_high(values)
-    )
+def spread_dot(table_value, parts):
+    slots, rows, columns = parts[0].shape
+    sides = []
+    for values in parts:
+        low, high = (
+            digit.reshape(slots * rows, columns).astype(jnp.bfloat16)
+            for digit in low_and_high(values)
+        )
+        sides.append(jnp.concatenate([low, high, low, high], axis=0))
     result = jnp.dot(
-        table_value,
-        jnp.concatenate([low, high, low, high], axis=0),
-        preferred_element_type=jnp.float32,
-    )
-    return result.reshape(-1, rows, columns)
+        table_value, jnp.concatenate(sides, axis=1), preferred_element_type=jnp.float32
+    )
+    return [
+        reduce_centred(
+            result[:, place * columns : (place + 1) * columns].reshape(-1, rows, columns)
+        )
+        for place in range(len(parts))
+    ]
 
 
 def as_float(values):
@@ -234,25 +241,26 @@
 
 def transform_group(table_ref, source_ref, block, start):
     values = as_float(source_ref[block, :, pl.ds(start, 2 * sub_rows), :])
-    table_value = table_ref[...]
-    return jnp.concatenate(
-        [
-            reduce_centred(spread_dot(table_value, values[:, :sub_rows])),
-            reduce_centred(spread_dot(table_value, values[:, sub_rows:])),
-        ],
-        axis=1,
-    )
-
-
-def digit_rows(start, chunk_rows):
-    top = start // chunk_rows * (2 * chunk_rows) + start % chunk_rows
-    return pl.multiple_of(top, sub_rows), pl.multiple_of(top + chunk_rows, sub_rows)
+    parts = [values[:, :sub_rows], values[:, sub_rows:]]
+    return jnp.concatenate(spread_dot(table_ref[...], parts), axis=1)
 
 
 def transform_left(table_ref, source_ref, block, chunk, count, digits_ref):
     columns = source_ref.shape[3]
-    chunk_rows = source_ref.shape[2] // chunk_count
-    groups = chunk_rows // (2 * sub_rows)
+    groups = source_ref.shape[2] // chunk_count // (2 * sub_rows)
+
+    def group(index, carry):
+        start = pl.multiple_of(index * 2 * sub_rows, 2 * sub_rows)
+        low, high = low_and_high(transform_group(table_ref, source_ref, block, start))
+        digits_ref[:, pl.ds(start, 2 * sub_rows), :columns] = high.astype(jnp.bfloat16)
+        digits_ref[:, pl.ds(start, 2 * sub_rows), columns:] = low.astype(jnp.bfloat16)
+        return carry
+
+    lax.fori_loop(chunk * groups, (chunk + count) * groups, group, 0)
+
+
+def transform_right(table_ref, source_ref, block, digits_ref):
+    rows, columns = source_ref.shape[2:]
 
     def group(index, carry):
         start = pl.multiple_of(index * 2 * sub_rows, 2 * sub_rows)
@@ -260,42 +268,22 @@
         low, high = low_and_high(values)
         shifted_low = jnp.round(values * (-1.0 / 96.0))
         shifted_high = values + 96.0 * shifted_low
-        top, bottom = (
-            pl.ds(pl.multiple_of(place, 2 * sub_rows), 2 * sub_rows)
-            for place in digit_rows(start, chunk_rows)
-        )
+        top, bottom = pl.ds(start, 2 * sub_rows), pl.ds(rows + start, 2 * sub_rows)
         digits_ref[:, top, :columns] = shifted_high.astype(jnp.bfloat16)
-        digits_ref[:, top, columns:] = high.astype(jnp.bfloat16)
-        digits_ref[:, bottom, :columns] = shifted_low.astype(jnp.bfloat16)
+        digits_ref[:, top, columns:] = shifted_low.astype(jnp.bfloat16)
+        digits_ref[:, bottom, :columns] = high.astype(jnp.bfloat16)
         digits_ref[:, bottom, columns:] = low.astype(jnp.bfloat16)
         return carry
 
-    lax.fori_loop(chunk * groups, (chunk + count) * groups, group, 0)
-
-
-def transform_right(table_ref, source_ref, block, digits_ref):
-    rows = source_ref.shape[2]
-
-    def group(index, carry):
-        start = pl.multiple_of(index * 2 * sub_rows, 2 * sub_rows)
-        values = transform_group(table_ref, source_ref, block, start)
-        low, high = low_and_high(values)
-        digits_ref[:, pl.ds(start, 2 * sub_rows), :] = high.astype(jnp.bfloat16)
-        digits_ref[:, pl.ds(rows + start, 2 * sub_rows), :] = low.astype(jnp.bfloat16)
-        return carry
-
     lax.fori_loop(0, rows // (2 * sub_rows), group, 0)
 
 
-point_unroll = 4
-
-
-def multiply_points(left_ref, right_ref, totals_ref, first, chunk=None):
-    if chunk is None:
-        rows = slice(None)
-    else:
-        count = left_ref.shape[1] // chunk_count
-        rows = pl.ds(pl.multiple_of(chunk * count, count), count)
+point_unroll = 8
+
+
+def multiply_points(left_ref, right_ref, totals_ref, first, part=None):
+    half = left_ref.shape[1] // 2
+    rows = slice(None) if part is None else pl.ds(pl.multiple_of(part * half, half), half)
 
     def point(index, carry):
         for place in range(point_unroll):
@@ -309,10 +297,10 @@
     lax.fori_loop(0, left_ref.shape[0] // point_unroll, point, 0)
 
 
-def folded(totals_ref, start, rows, chunk_rows):
-    top, bottom = digit_rows(start, chunk_rows)
-    high = totals_ref[:, pl.ds(top, rows), :]
-    low = totals_ref[:, pl.ds(bottom, rows), :]
+def folded(totals_ref, start, rows):
+    width = totals_ref.shape[2] // 2
+    high = totals_ref[:, pl.ds(start, rows), :width]
+    low = totals_ref[:, pl.ds(start, rows), width:]
     values = reduce_centred(reduce_centred(high) * 128.0 + low)
     half = values.shape[0] // 2
     return values[:half] + values[half:], values[:half] - values[half:]
@@ -485,8 +473,11 @@
     def last(chunk):
         line.tick(line.size - 2, chunk)
         left(line.block_at(line.size - 1), chunk, 1)
-        multiply(False, chunk)
-        finish(chunk)
+
+        @pl.when(chunk % 2 == 1)
+        def _():
+            multiply(False, chunk // 2)
+            finish(chunk // 2)
 
     each_chunk(last)
     line.finish()
@@ -525,28 +516,24 @@
     for copy in copies:
         copy.wait()
     each_chunk(lambda chunk: (line.start(chunk), square.start(chunk)))
-    chunk_rows = line.rows
-    groups = chunk_rows // (2 * sub_rows)
-
-    def finish(chunk):
+    groups = out_ref.shape[1] // 2 // (2 * sub_rows)
+
+    def finish(part):
         def group(index, carry):
             start = pl.multiple_of(index * 2 * sub_rows, 2 * sub_rows)
-            halves = []
-            for half in range(2):
-                sums, differences = folded(totals, start + half * sub_rows, sub_rows, chunk_rows)
-                halves.append(
-                    [
-                        reduce_centred(spread_dot(even_ref[...], sums)),
-                        reduce_centred(spread_dot(odd_ref[...], differences)),
-                    ]
+            halves = zip(
+                *(
+                    folded(totals, start + half * sub_rows, sub_rows)
+                    for half in range(2)
                 )
-            for parity in range(2):
-                values = as_short(jnp.concatenate([halves[0][parity], halves[1][parity]], axis=1))
+            )
+            for parity, (table_ref, parts) in enumerate(zip((even_ref, odd_ref), halves)):
+                values = as_short(jnp.concatenate(spread_dot(table_ref[...], parts), axis=1))
                 for place in range(values.shape[0]):
                     out_ref[2 * place + parity, pl.ds(start, 2 * sub_rows), :] = values[place]
             return carry
 
-        lax.fori_loop(chunk * groups, (chunk + 1) * groups, group, 0)
+        lax.fori_loop(part * groups, (part + 1) * groups, group, 0)
 
     pipeline(
         line,
@@ -635,22 +622,24 @@
         each_chunk(square.start)
         each_chunk(lambda chunk: (cross_left(chunk).wait_recv(), line.start(chunk)))
 
-    chunk_rows = line.rows
-    groups = chunk_rows // sub_rows
-
-    def finish(chunk):
+    groups = out_ref.shape[1] // 2 // (2 * sub_rows)
+
+    def finish(part):
         def group(index, carry):
-            start = pl.multiple_of(index * sub_rows, sub_rows)
-            for parity, (table_ref, values) in enumerate(
-                zip((even_ref, odd_ref), folded(totals, start, sub_rows, chunk_rows))
-            ):
-                result = reduce_centred(spread_dot(table_ref[...], values))
-                result = jnp.where(result < 0.0, result + 12289.0, result) * (1.0 / 12289.0)
-                for place in range(result.shape[0]):
-                    out_ref[2 * place + parity, pl.ds(start, sub_rows), :] = result[place]
+            start = pl.multiple_of(index * 2 * sub_rows, 2 * sub_rows)
+            halves = zip(
+                *(
+                    folded(totals, start + half * sub_rows, sub_rows)
+                    for half in range(2)
+                )
+            )
+            for parity, (table_ref, parts) in enumerate(zip((even_ref, odd_ref), halves)):
+                values = as_short(jnp.concatenate(spread_dot(table_ref[...], parts), axis=1))
+                for place in range(values.shape[0]):
+                    out_ref[2 * place + parity, pl.ds(start, 2 * sub_rows), :] = values[place]
             return carry
 
-        lax.fori_loop(chunk * groups, (chunk + 1) * groups, group, 0)
+        lax.fori_loop(part * groups, (part + 1) * groups, group, 0)
 
     pipeline(
         line,
@@ -664,22 +653,22 @@
     pl.when(side == 1)(lambda: each_chunk(lambda chunk: cross_right(chunk).wait_send()))
 
 
-def call(kernel, collective_id, arguments, tables, out_shape, out_dtype, shapes, extra=()):
+def call(kernel, collective_id, arguments, tables, out_shape, shapes, extra=()):
     left, right, points = shapes
     size, rows, columns = left[0], left[2], left[3]
     inner, width = right[2], right[3]
     return pl.pallas_call(
         functools.partial(kernel, size),
-        out_shape=jax.ShapeDtypeStruct(out_shape, out_dtype),
+        out_shape=jax.ShapeDtypeStruct(out_shape, jnp.int16),
         in_specs=[pl.BlockSpec(memory_space=pl.ANY)] * len(arguments)
         + [pl.BlockSpec(memory_space=pltpu.VMEM)] * len(tables),
         out_specs=pl.BlockSpec(memory_space=pltpu.VMEM),
         scratch_shapes=[
             pltpu.VMEM(left, jnp.int16),
             pltpu.VMEM(right, jnp.int16),
-            pltpu.VMEM((points, 2 * rows, 2 * columns), jnp.bfloat16),
-            pltpu.VMEM((points, 2 * inner, width), jnp.bfloat16),
-            pltpu.VMEM((points, 2 * rows, width), jnp.float32),
+            pltpu.VMEM((points, rows, 2 * columns), jnp.bfloat16),
+            pltpu.VMEM((points, 2 * inner, 2 * width), jnp.bfloat16),
+            pltpu.VMEM((points, rows, 2 * width), jnp.float32),
             pltpu.SemaphoreType.DMA((2, size - 1, chunk_count)),
             pltpu.SemaphoreType.DMA((2, size - 1, chunk_count)),
             pltpu.SemaphoreType.DMA((3, chunk_count)),
@@ -710,14 +699,13 @@
             spread_table(inverse_one[1::2, :slots]),
         ],
         (points, rows, columns),
-        jnp.int16,
         ((size, slots, rows, columns), (size, slots, rows, columns), points),
     )
     last_points = 3 * slots
     inverse_two = make_table(last_points, last_points - 3, last_points, True)
     half = last_points // 2
     own_rows = rows // lax.axis_size("pt")
-    return call(
+    result = call(
         result_kernel,
         1,
         (products,),
@@ -728,13 +716,14 @@
             spread_table(inverse_two[1::2, :half]),
         ],
         (last_points - 3, own_rows, columns),
-        jnp.float32,
         ((size, points, own_rows, columns), (size, slots, rows, columns), last_points),
         extra=(
             pltpu.SemaphoreType.DMA((chunk_count,)),
             pltpu.SemaphoreType.DMA((chunk_count,)),
         ),
     )
+    result = result.astype(jnp.float32)
+    return jnp.where(result < 0.0, result + 12289.0, result) / 12289.0
 
 
 def solution(mesh):

time: 343 us -> 333 us (0.971)
  Pallas kernels: 331 us -> 320 us
  local copies, waits for them, and re-layouts: 5.93 us -> 0 us
  other arithmetic: 6.58 us -> 12.5 us
    pallas_call x2, Pallas kernels: 331 us -> 320 us  [call(): pl.pallas_call(functools.partial(kernel, size), out_shape=jax.ShapeDtypeS...]
    unnamed x1 -> x0, local copies, waits for them, and re-layouts: 5.93 us -> none
    div x0 -> x1, other arithmetic: none -> 5.93 us  [square_local(): return jnp.where(result < 0.0, result + 12289.0, result) / 12289.0]
where the time goes in v3:
time: 333 us
  Pallas kernels  320 us (96%)
  other arithmetic  12.5 us (4%)
    pallas_call x2, Pallas kernels, call(): pl.pallas_call(functools.partial(kernel, size), out_shape=jax.ShapeDtypeS...  320 us

profile of v3, /device:TPU:4, one launch (start us, length us, event | category | flops | bytes accessed | tf_op | source)
XLA Modules:
  0.0 332.6 jit_solution(17613144422818694601)
XLA Ops:
  0.0 6.6 %fusion.1 = (s16[16,256,256]{2,1,0:T(8,128)(2,1)}, s16[16,256,256]{2,1,0:T(8,128)(2,1)}) fusion(s32[16,256,256]{2,1,0:T(8,128)} %param.9, s32[16,256,256]{2,1,0:T(8,128)} %param.10), kind=kLoop, calls=%fused_computation.4 | loop fusion | flops 8388608 | bytes 12582912 | tf_op jit(solution)/shard_map/convert_element_type | solution.py:691
  6.6 152.0 %product_kernel.1.product_hbm = s16[32,256,256]{2,1,0:T(8,128)(2,1)} custom-call(s16[16,256,256]{2,1,0:T(8,128)(2,1)} %get-tuple-element.5.left_hbm, s16[16,256,256]{2,1,0:T(8,128)(2,1)} %get-tuple-element.6.right_hbm, bf16[256,512]{1,0:T(8,128)(2,1)} %constant.26.clone.forward_ref, bf16[128,512]{1,0:T(8,128)(2,1)} %constant.27.clone.even_ref, ...), custom_call_target="tpu_custom_call" | custom-call | tf_op jit(solution)/shard_map/product_kernel/pallas_call | solution.py:660
  158.6 168.1 %result_kernel.1 = s16[45,128,256]{2,1,0:T(8,128)(2,1)} custom-call(s16[32,256,256]{2,1,0:T(8,128)(2,1)} %product_kernel.1.product_hbm, bf16[384,1024]{1,0:T(8,128)(2,1)} %constant.29.clone.upper_table, bf16[384,512]{1,0:T(8,128)(2,1)} %constant.30.clone.lower_table, bf16[184,768]{1,0:T(8,128)(2,1)} %constant.31.clone.even_ref, ...), custom_call_target="tpu_custom_call" | custom-call | tf_op jit(solution)/shard_map/result_kernel/pallas_call | solution.py:660
  326.7 5.9 %fusion = f32[45,128,256]{2,1,0:T(8,128)} fusion(s16[45,128,256]{2,1,0:T(8,128)(2,1)} %result_kernel.1), kind=kLoop, calls=%fused_computation.3 | loop fusion | flops 7372800 | bytes 8847360 | tf_op jit(solution)/shard_map/div | solution.py:726

commit v4 on v3

--- a/solution.py
+++ b/solution.py
@@ -189,7 +189,7 @@
 
 MESH = pl.DeviceIdType.MESH
 sub_rows = 8
-chunk_count = 4
+chunk_count = 8
 vmem_limit = 67_000_000
 
 
@@ -278,23 +278,21 @@
     lax.fori_loop(0, rows // (2 * sub_rows), group, 0)
 
 
-point_unroll = 8
-
-
 def multiply_points(left_ref, right_ref, totals_ref, first, part=None):
     half = left_ref.shape[1] // 2
     rows = slice(None) if part is None else pl.ds(pl.multiple_of(part * half, half), half)
+    unroll = 4 if part is None else 8
 
     def point(index, carry):
-        for place in range(point_unroll):
-            at = index * point_unroll + place
+        for place in range(unroll):
+            at = index * unroll + place
             product = jnp.dot(
                 left_ref[at, rows, :], right_ref[at], preferred_element_type=jnp.float32
             )
             totals_ref[at, rows, :] = product if first else totals_ref[at, rows, :] + product
         return carry
 
-    lax.fori_loop(0, left_ref.shape[0] // point_unroll, point, 0)
+    lax.fori_loop(0, left_ref.shape[0] // unroll, point, 0)
 
 
 def folded(totals_ref, start, rows):
@@ -456,15 +454,24 @@
 
     each_chunk(first)
     each_chunk(square.arrive)
-    line.tick(1, 0)
+    quarter = chunk_count // 4
+
+    def pass_on(index):
+        def one(chunk, carry):
+            line.tick(1, chunk)
+            return carry
+
+        lax.fori_loop(index * quarter, (index + 1) * quarter, one, 0)
+
+    pass_on(0)
     right(line.block_at(0))
     multiply(True)
-    line.tick(1, 1)
+    pass_on(1)
     left(line.block_at(1), 0, chunk_count)
     right(line.block_at(1))
-    line.tick(1, 2)
+    pass_on(2)
     multiply(False)
-    line.tick(1, 3)
+    pass_on(3)
     left(line.block_at(2), 0, chunk_count)
     right(line.block_at(2))
     multiply(False)
@@ -474,10 +481,12 @@
         line.tick(line.size - 2, chunk)
         left(line.block_at(line.size - 1), chunk, 1)
 
-        @pl.when(chunk % 2 == 1)
+        half = chunk_count // 2
+
+        @pl.when(chunk % half == half - 1)
         def _():
-            multiply(False, chunk // 2)
-            finish(chunk // 2)
+            multiply(False, chunk // half)
+            finish(chunk // half)
 
     each_chunk(last)
     line.finish()
@@ -501,21 +510,38 @@
     line_receive,
     square_send,
     square_receive,
+    staged,
     local_sems,
 ):
     slots = left_ref.shape[1]
     line = Line("col", size, left_ref, slots, line_send, line_receive)
     square = Square("row", right_ref, slots, square_send, square_receive)
-    copies = (
-        pltpu.make_async_copy(left_hbm, left_ref.at[line.place], local_sems.at[0]),
-        pltpu.make_async_copy(right_hbm, right_ref.at[square.place], local_sems.at[1]),
-    )
-    for copy in copies:
-        copy.start()
+    inputs = ((left_hbm, left_ref, line), (right_hbm, right_ref, square))
+
+    def load(side, chunk):
+        source, _, ring = inputs[side]
+        rows = pl.ds(pl.multiple_of(chunk * ring.rows, ring.rows), ring.rows)
+        return pltpu.make_async_copy(source.at[:, rows, :], staged.at[side], local_sems.at[side])
+
+    load(0, 0).start()
+    load(1, 0).start()
     greet(line, square)
-    for copy in copies:
-        copy.wait()
-    each_chunk(lambda chunk: (line.start(chunk), square.start(chunk)))
+
+    def own(chunk):
+        for side, (_, target, ring) in enumerate(inputs):
+            load(side, chunk).wait()
+            rows = pl.ds(pl.multiple_of(chunk * ring.rows, ring.rows), ring.rows)
+            target[ring.place, :, rows, :] = centre(staged[side]).astype(jnp.int16)
+            pl.when(chunk + 1 < chunk_count)(lambda side=side: load(side, chunk + 1).start())
+
+        @pl.when(chunk > 0)
+        def _():
+            line.start(chunk - 1)
+            square.start(chunk - 1)
+
+    each_chunk(own)
+    line.start(chunk_count - 1)
+    square.start(chunk_count - 1)
     groups = out_ref.shape[1] // 2 // (2 * sub_rows)
 
     def finish(part):
@@ -688,11 +714,10 @@
     slots, rows, columns = first_factors.shape
     points = 2 * slots
     inverse_one = make_table(points, points, points, True)
-    left, right = (centre(values).astype(jnp.int16) for values in (first_factors, second_factors))
     products = call(
         product_kernel,
         0,
-        (left, right),
+        (first_factors, second_factors),
         [
             spread_table(make_table(points, points, slots, False)),
             spread_table(inverse_one[0::2, :slots]),
@@ -700,6 +725,7 @@
         ],
         (points, rows, columns),
         ((size, slots, rows, columns), (size, slots, rows, columns), points),
+        extra=(pltpu.VMEM((2, slots, rows // chunk_count, columns), jnp.int32),),
     )
     last_points = 3 * slots
     inverse_two = make_table(last_points, last_points - 3, last_points, True)

time: 333 us -> 329 us (0.988)
  other arithmetic: 12.5 us -> 5.93 us
    convert_element_type x1 -> x0, other arithmetic: 6.55 us -> none  [square_local(): centre(values).astype(jnp.int16)]
where the time goes in v4:
time: 329 us
  Pallas kernels  323 us (98%)
  other arithmetic  5.93 us (2%)
    pallas_call x2, Pallas kernels, call(): pl.pallas_call(functools.partial(kernel, size), out_shape=jax.ShapeDtypeS...  323 us

profile of v4, /device:TPU:4, one launch (start us, length us, event | category | flops | bytes accessed | tf_op | source)
XLA Modules:
  0.0 328.7 jit_solution(1184827894546871895)
XLA Ops:
  0.0 154.5 %product_kernel.1.product_hbm = s16[32,256,256]{2,1,0:T(8,128)(2,1)} custom-call(s32[16,256,256]{2,1,0:T(8,128)} %left_hbm.1, s32[16,256,256]{2,1,0:T(8,128)} %right_hbm.1, bf16[256,512]{1,0:T(8,128)(2,1)} %constant.20.clone.forward_ref, bf16[128,512]{1,0:T(8,128)(2,1)} %constant.21.clone.even_ref, bf16[128,512]{1,0:T(8,128)(2,1)} %constant.22.clone.odd_ref), custom_call_target="tpu_custom_call" | custom-call | tf_op jit(solution)/shard_map/product_kernel/pallas_call | solution.py:686
  154.5 168.3 %result_kernel.1 = s16[45,128,256]{2,1,0:T(8,128)(2,1)} custom-call(s16[32,256,256]{2,1,0:T(8,128)(2,1)} %product_kernel.1.product_hbm, bf16[384,1024]{1,0:T(8,128)(2,1)} %constant.23.clone.upper_table, bf16[384,512]{1,0:T(8,128)(2,1)} %constant.24.clone.lower_table, bf16[184,768]{1,0:T(8,128)(2,1)} %constant.25.clone.even_ref, ...), custom_call_target="tpu_custom_call" | custom-call | tf_op jit(solution)/shard_map/result_kernel/pallas_call | solution.py:686
  322.7 5.9 %fusion = f32[45,128,256]{2,1,0:T(8,128)} fusion(s16[45,128,256]{2,1,0:T(8,128)(2,1)} %result_kernel.1), kind=kLoop, calls=%fused_computation.1 | loop fusion | flops 7372800 | bytes 8847360 | tf_op jit(solution)/shard_map/div | solution.py:752
